TPU v7x, 512 devices: a 4x2x32 block of a 4x8x32 slice. The times are simulated.
512 devices in a mesh: grp: 2 (over y), sp: 128 (over x, z), ch: 2 (over core).
Axes of the slice: x: 4, y: 2, z: 32, core: 2. Of those that a mesh axis runs over, the one named last changes fastest.
The devices are a block of a 4x8x32 slice.
Arguments:
- latents: bfloat16 [262144, 1024], P(('grp', 'sp')), parts along dimension 0, may hold values from -6 to 6
- spectrum: bfloat16 [16, 64, 128, 1024], P(None, None, 'sp', 'ch'), may hold values from -4 to 4
- w_value: bfloat16 [1024, 1024], P('sp', 'ch'), may hold values from -0.1875 to 0.1875
- w_gate: bfloat16 [1024, 1024], P('sp', 'ch'), may hold values from -0.1875 to 0.1875
- w_out: bfloat16 [1024, 1024], P('sp'), may hold values from -0.1875 to 0.1875
- embed_table: bfloat16 [1024, 32768], P(('sp', 'ch')), may hold values from -12 to 12
- prompt_ids: int32 [512], P('grp'), parts along dimension 0, may hold values from 0 to 32767
- noise_step: int32 [2], P('grp'), parts along dimension 0, may hold values from 0 to 999
Outputs:
- denoised: bfloat16 [262144, 1024], P(('grp', 'sp', 'ch')), parts along dimension 0
There are 2 independent parts, one for each index of `grp`. A program takes and returns all parts, laid end to end along the dimension named above; an argument that names none is the same for every part. Nothing has to cross between parts.
All inputs are finite; a program needn't handle non-finite values.
Results may differ from a plain program's by a relative error of at most 0.013.
Values may be sent and summed in bfloat16 or wider, within the bound.
A program may use at most 64 MiB of HBM per device.

v0:
```python
import math
import jax
import jax.numpy as jnp
from jax import lax
from jax.sharding import Mesh
from jax.sharding import PartitionSpec as P

TT = 16
HH = 64
WW = 128
C = 1024
SP = ("sp_0", "sp_1")
SP_CH = ("sp_0", "sp_1", "ch")
GRP_SP = ("grp", "sp_0", "sp_1")
GRP_SP_CH = ("grp", "sp_0", "sp_1", "ch")
F32 = jnp.float32
BF16 = jnp.bfloat16


def cas_table(length):
    position = jnp.arange(length, dtype=jnp.int32)
    product = position[:, None] * position[None, :] % length
    phase_angle = product.astype(jnp.float32) * (2.0 * math.pi / length)
    return ((jnp.cos(phase_angle) + jnp.sin(phase_angle)) / math.sqrt(length)).astype(jnp.bfloat16)


def step_embedding(noise_step, channel, channels):
    half_count = channels // 2
    lower_half = channel < half_count
    position = jnp.where(lower_half, channel, channel - half_count).astype(jnp.float32)
    frequency = jnp.exp(-math.log(10000.0) * position / half_count)
    phase_angle = noise_step[0].astype(jnp.float32) * frequency
    return jnp.where(lower_half, jnp.sin(phase_angle), jnp.cos(phase_angle))


def dot(a, b):
    return jnp.dot(a, b, preferred_element_type=F32)


def local_pool(embed_table, prompt_ids):
    vocab = embed_table.shape[1]
    low = 256
    high_hot = (prompt_ids[:, None] // low == jnp.arange(vocab // low)[None, :]).astype(BF16)
    low_hot = (prompt_ids[:, None] % low == jnp.arange(low)[None, :]).astype(BF16)
    counts = jnp.einsum("ph,pl->hl", high_hot, low_hot, preferred_element_type=F32)
    total = jnp.sum(embed_table.astype(F32) * counts.reshape(1, vocab), axis=1)
    return total / prompt_ids.shape[0]


def local(latents, spectrum, w_value, w_gate, w_out, embed_table, prompt_ids, noise_step):
    row_count = latents.shape[0]
    part = w_value.shape[1]
    lines = row_count // WW
    core = lax.axis_index("ch")
    offset = core * part
    pool4 = local_pool(embed_table, prompt_ids)
    pool8 = lax.all_gather(pool4, "ch", axis=0, tiled=True)
    high = lax.reduce_precision(pool8, 8, 7)
    low = pool8 - high
    pool_cols = jnp.pad(jnp.stack([high, low], axis=1), ((0, 0), (0, 126))).astype(BF16)
    packed = jnp.concatenate([w_value, w_gate, w_out, pool_cols], axis=1)
    column = lax.all_gather(packed, "sp_1", axis=0, tiled=True)
    weights = lax.all_gather(column, "sp_0", axis=0, tiled=True)
    cas_width = cas_table(WW)
    space = jnp.einsum("st,ah->sath", cas_table(TT).astype(F32), cas_table(HH).astype(F32))
    space = space.reshape(TT * HH, TT * HH).astype(BF16)
    mine = lax.dynamic_slice_in_dim(latents, offset, part, 1).reshape(lines, WW, part)
    spread = jnp.einsum("kw,lwc->klc", cas_width, mine, preferred_element_type=F32).astype(BF16)
    arrived = lax.all_to_all(spread, SP, split_axis=0, concat_axis=0, tiled=True)
    arrived = arrived.reshape(TT * HH, part)
    both = lax.all_gather(arrived, "ch", axis=1, tiled=True)
    width_spec = dot(both, weights[:, :part]).astype(BF16)
    full_spec = dot(space, width_spec).astype(BF16)
    gains = spectrum.reshape(TT * HH, part)
    filtered = (full_spec.astype(F32) * gains.astype(F32)).astype(BF16)
    height_back = dot(space, filtered).astype(BF16)
    returned = lax.all_to_all(
        height_back.reshape(-1, lines, part), SP, split_axis=0, concat_axis=0, tiled=True
    )
    gate_rows = dot(latents, weights[:, part : 2 * part])
    pooled_all = weights[:, 2 * part + C].astype(F32) + weights[:, 2 * part + C + 1].astype(F32)
    pooled = lax.dynamic_slice_in_dim(pooled_all, offset, part)
    channel = offset + jnp.arange(part, dtype=jnp.int32)
    modulation = 1.0 + pooled + step_embedding(noise_step, channel, C)
    gain = jax.nn.silu(gate_rows) * modulation[None, :]
    mix_rows = jnp.einsum("wk,klc->lwc", cas_width, returned, preferred_element_type=F32)
    mixed = (mix_rows.reshape(row_count, part) * gain).astype(BF16)
    half = row_count // lax.axis_size("ch")
    moved = lax.all_to_all(mixed, "ch", split_axis=0, concat_axis=1, tiled=True)
    summed = dot(moved, weights[:, 2 * part : 2 * part + C])
    residual = lax.dynamic_slice_in_dim(latents, core * half, half, 0)
    return (residual.astype(F32) + summed).astype(BF16)


def solution(mesh):
    torus = Mesh(
        mesh.devices.reshape(mesh.shape["grp"], 4, 32, mesh.shape["ch"]),
        ("grp", "sp_0", "sp_1", "ch"),
    )
    in_specs = (
        P(GRP_SP, None),
        P(None, None, SP, "ch"),
        P(SP, "ch"),
        P(SP, "ch"),
        P(SP, None),
        P(SP_CH, None),
        P("grp"),
        P("grp"),
    )
    out_specs = P(GRP_SP_CH, None)
    return jax.shard_map(local, mesh=torus, in_specs=in_specs, out_specs=out_specs, check_vma=False)
```

profile of v0, /device:TPU:33, one launch (start us, length us, event | category | flops | bytes accessed | tf_op | source)
XLA Modules:
  0.0 464.0 jit_solution(6335007486320289089)
XLA Ops:
  6.6 0.7 and_select_fusion.1
  7.6 1.3 dynamic-slice.1
  9.5 1.3 multiply_reduce_fusion
  11.0 43.6 %all-reduce.1 = f32[8]{0:T(128)S(1)} all-reduce(f32[8]{0:T(128)S(1)} %multiply_dynamic-update-slice_fusion), channel_id=1, replica_groups=mesh['grp'=2,'sp_0'=4,'sp_1'=32,'ch'=2] {'ch'}, use_global_device_ids=true, to_apply=%add.1 | all-reduce | flops 8 | bytes 64
  54.7 1.4 fusion.28
  56.1 1.3 constant_dynamic-slice_fusion
  58.1 1.5 copy.17
  59.6 12.9 %all-to-all-start = ((bf16[128,8,512]{2,1,0:T(8,128)(2,1)}), bf16[128,8,512]{2,1,0:T(8,128)(2,1)S(1)}, u32[]{:S(2)}, u32[]{:S(2)}) async-start(bf16[128,8,512]{2,1,0:T(8,128)(2,1)} %copy.17), calls=%async_computation | async-start | bytes 2097152 | tf_op jit(solution)/shard_map/all_to_all | solution.py:69
  72.6 118.9 %all-gather.6.cloned.1.call-done = bf16[256,2176]{1,0:T(8,128)(2,1)} async-done(((bf16[8,2176]{1,0:T(8,128)(2,1)}), bf16[256,2176]{1,0:T(8,128)(2,1)}) %all-gather.6.cloned.1.call-update) | async-done | bytes 1114128 | tf_op jit(solution)/shard_map/all_gather | solution.py:62
  191.7 1.0 copy-done
  192.9 3.0 fusion
  195.9 5.6 %convert_element_type.98 = bf16[1024,1024]{1,0:T(8,128)(2,1)S(1)} reshape(bf16[16,64,16,64]{3,2,1,0:T(8,128)(2,1)} %fusion) | data formatting | bytes 4194304 | tf_op jit(solution)/shard_map/convert_element_type | solution.py:66
  201.4 62.7 %all-gather.8.cloned.1.call-done = bf16[1024,2176]{1,0:T(8,128)(2,1)} async-done(((bf16[256,2176]{1,0:T(8,128)(2,1)}), bf16[1024,2176]{1,0:T(8,128)(2,1)}) %all-gather.8.cloned.1.call-update) | async-done | bytes 4456464 | tf_op jit(solution)/shard_map/all_gather | solution.py:63
  264.2 35.1 %all-gather.4.cloned.1.call-done = bf16[1024,1024]{1,0:T(8,128)(2,1)} async-done(((bf16[1024,512]{1,0:T(8,128)(2,1)}), bf16[1024,1024]{1,0:T(8,128)(2,1)}) %all-gather.4.cloned.1.call-update) | async-done | bytes 2097168 | tf_op jit(solution)/shard_map/all_gather | solution.py:71
  299.3 5.2 %fusion.3 = bf16[1024,512]{1,0:T(8,128)(2,1)} fusion(bf16[1024,512]{1,0:T(8,128)(2,1)S(1)} %bitcast.64, bf16[1024,1024]{1,0:T(8,128)(2,1)S(1)} %convert_element_type.98, bf16[1024,1024]{1,0:T(8,128)(2,1)} %all-gather.4.cloned.1.call-done, bf16[1024,2176]{1,0:T(8,128)(2,1)} %all-gather.8.cloned.1.call-done), kind=kOutput, calls=%fused_computation.5 | convolution fusion | flops 2150629376 | bytes 7340032 | tf_op jit(solution)/shard_map/dot_general | solution.py:37
  304.5 3.5 fusion.12
  307.9 28.1 %all-to-all-start.1 = ((bf16[128,8,512]{2,1,0:T(8,128)(2,1)}), bf16[128,8,512]{2,1,0:T(8,128)(2,1)S(1)}, u32[]{:S(2)}, u32[]{:S(2)}) async-start(bf16[128,8,512]{2,1,0:T(8,128)(2,1)} %fusion.12), calls=%async_computation.1 | async-start | bytes 2097152 | tf_op jit(solution)/shard_map/all_to_all | solution.py:77
  336.7 1.2 fusion.70
  338.1 101.6 %all-to-all-done.1 = bf16[128,8,512]{2,1,0:T(8,128)(2,1)S(1)} async-done(((bf16[128,8,512]{2,1,0:T(8,128)(2,1)}), bf16[128,8,512]{2,1,0:T(8,128)(2,1)S(1)}, u32[]{:S(2)}, u32[]{:S(2)}) %all-to-all-start.1) | async-done | bytes 1048608 | tf_op jit(solution)/shard_map/all_to_all | solution.py:77
  439.7 1.1 fusion.15
  440.8 1.9 copy.20
  442.6 4.2 fusion.9
  446.9 6.7 %all_to_all.29 = bf16[2,512,512]{1,2,0:T(8,128)(2,1)S(1)} all-to-all(bf16[2,512,512]{1,2,0:T(8,128)(2,1)S(1)} %bitcast.60), channel_id=1, replica_groups=mesh['grp'=2,'sp_0'=4,'sp_1'=32,'ch'=2] {'ch'}, dimensions={0} | all-to-all | bytes 2097152 | tf_op jit(solution)/shard_map/all_to_all | solution.py:89
  453.6 3.8 add_convert_fusion
  (25 shorter events, 2.0 us)
Async XLA Ops:
  6.5 185.0 %all-gather.6.cloned.1.call-start = ((), (), s32[]{:S(2)}) async-start(), calls=%async_computation.4 | async-start | bytes 1148928 | tf_op jit(solution)/shard_map/all_gather | solution.py:62
  59.6 132.0 %all-to-all-start = ((bf16[128,8,512]{2,1,0:T(8,128)(2,1)}), bf16[128,8,512]{2,1,0:T(8,128)(2,1)S(1)}, u32[]{:S(2)}, u32[]{:S(2)}) async-start(bf16[128,8,512]{2,1,0:T(8,128)(2,1)} %copy.17), calls=%async_computation | async-start | bytes 2097152 | tf_op jit(solution)/shard_map/all_to_all | solution.py:69
  72.5 191.7 %all-gather.8.cloned.1.call-start = ((), (), s32[]{:S(2)}) async-start(), calls=%async_computation.5 | async-start | bytes 5570560 | tf_op jit(solution)/shard_map/all_gather | solution.py:63
  191.6 107.7 %all-gather.4.cloned.1.call-start = ((), (), s32[]{:S(2)}) async-start(), calls=%async_computation.3 | async-start | bytes 3145728 | tf_op jit(solution)/shard_map/all_gather | solution.py:71
  191.7 1.0 copy-start
  195.9 103.4 %copy-start.2 = (bf16[16,64,1,512]{3,1,2,0:T(8,128)(2,1)S(1)}, bf16[16,64,1,512]{3,1,2,0:T(8,128)(2,1)}, u32[]{:S(2)}) copy-start(bf16[16,64,1,512]{3,1,2,0:T(8,128)(2,1)} %param.9) | copy-start | bytes 3145732
  307.9 131.8 %all-to-all-start.1 = ((bf16[128,8,512]{2,1,0:T(8,128)(2,1)}), bf16[128,8,512]{2,1,0:T(8,128)(2,1)S(1)}, u32[]{:S(2)}, u32[]{:S(2)}) async-start(bf16[128,8,512]{2,1,0:T(8,128)(2,1)} %fusion.12), calls=%async_computation.1 | async-start | bytes 2097152 | tf_op jit(solution)/shard_map/all_to_all | solution.py:77
  446.8 6.8 %copy-start.1 = (bf16[1024,1024]{1,0:T(8,128)(2,1)S(1)}, bf16[1024,1024]{1,0:T(8,128)(2,1)}, u32[]{:S(2)}) copy-start(bf16[1024,1024]{1,0:T(8,128)(2,1)} %param.8) | copy-start | bytes 6291460
Sparse Core Ops, SparseCore 0:
  56.2 135.2 all-gather.5
  193.6 70.4 all-gather.7
  266.3 32.9 all-gather.3
where the time goes:
time: 465 us; the launch traced here: 464 us
  waiting for transfers between devices  319 us (69%)
  blocking collectives  50.3 us (11%)
  starting transfers between devices  41.1 us (9%)
  matrix products  18.7 us (4%)
  between operations  14.6 us (3%)
  local copies, waits for them, and re-layouts  13.9 us (3%)
  other arithmetic  6.88 us (1%)
    all_gather x1, waiting for transfers between devices, local(): column = lax.all_gather(packed, 'sp_1', axis=0, tiled=True)  119 us
    all_to_all x1, waiting for transfers between devices, local(): lax.all_to_all(height_back.reshape(-1, lines, part), SP, split_axis=0, co...  102 us
    all_gather x1, waiting for transfers between devices, local(): weights = lax.all_gather(column, 'sp_0', axis=0, tiled=True)  62.7 us
    unnamed x1, blocking collectives  43.6 us
    all_gather x1, waiting for transfers between devices, local(): both = lax.all_gather(arrived, 'ch', axis=1, tiled=True)  35.1 us
    all_to_all x1, starting transfers between devices, local(): lax.all_to_all(height_back.reshape(-1, lines, part), SP, split_axis=0, co...  28.1 us
    dot_general x4, matrix products, dot(): return jnp.dot(a, b, preferred_element_type=F32)  16.7 us
    all_to_all x1, starting transfers between devices, local(): lax.all_to_all(spread, SP, split_axis=0, concat_axis=0, tiled=True)  12.9 us
  transfers between devices with their start and end apart: 5, of which 4 were waited for; matrix products, arithmetic and copies ran while one was open for 3% of the time, Pallas kernels for 0%

commit v1 on v0

--- a/solution.py
+++ b/solution.py
@@ -60,7 +60,9 @@
     pool_cols = jnp.pad(jnp.stack([high, low], axis=1), ((0, 0), (0, 126))).astype(BF16)
     packed = jnp.concatenate([w_value, w_gate, w_out, pool_cols], axis=1)
     column = lax.all_gather(packed, "sp_1", axis=0, tiled=True)
-    weights = lax.all_gather(column, "sp_0", axis=0, tiled=True)
+    weights = jnp.concatenate(
+        lax.all_to_all(jnp.stack([column] * lax.axis_size("sp_0")), "sp_0", 0, 0), axis=0
+    )
     cas_width = cas_table(WW)
     space = jnp.einsum("st,ah->sath", cas_table(TT).astype(F32), cas_table(HH).astype(F32))
     space = space.reshape(TT * HH, TT * HH).astype(BF16)

time: 465 us -> 426 us (0.916)
  waiting for transfers between devices: 319 us -> 256 us
  starting transfers between devices: 41.1 us -> 84.6 us
  blocking collectives: 50.3 us -> 21 us
  local copies, waits for them, and re-layouts: 13.9 us -> 23.5 us
    all_gather x1 -> x0, waiting for transfers between devices: 62.7 us -> none  [local(): weights = lax.all_gather(column, 'sp_0', axis=0, tiled=True)]
    all_to_all x1, starting transfers between devices: 12.9 us -> 53.7 us  [local(): lax.all_to_all(spread, SP, split_axis=0, concat_axis=0, tiled=True)]
    unnamed x1, blocking collectives: 43.6 us -> 3.02 us
    all_gather x1, waiting for transfers between devices: 35.1 us -> 0.01 us  [local(): both = lax.all_gather(arrived, 'ch', axis=1, tiled=True)]
    all_to_all x0 -> x1, waiting for transfers between devices: none -> 27.5 us  [local(): lax.all_to_all(jnp.stack([column] * lax.axis_size('sp_0')), 'sp_0', 0, 0)]
    all_gather x1, waiting for transfers between devices: 119 us -> 137 us  [local(): column = lax.all_gather(packed, 'sp_1', axis=0, tiled=True)]
    all_to_all x1, blocking collectives: 6.7 us -> 18 us  [local(): moved = lax.all_to_all(mixed, 'ch', split_axis=0, concat_axis=1, tiled=True)]
    all_to_all x1, waiting for transfers between devices: 102 us -> 91.3 us  [local(): lax.all_to_all(height_back.reshape(-1, lines, part), SP, split_axis=0, co...]
  transfers between devices with their start and end apart: 5 -> 5, of which waited for: 4 -> 3; matrix products, arithmetic and copies ran while one was open for 3% -> 5% of each run, Pallas kernels for 0% -> 0%
where the time goes in v1:
time: 426 us; the launch traced here: 425 us
  waiting for transfers between devices  256 us (60%)
  starting transfers between devices  84.6 us (20%)
  local copies, waits for them, and re-layouts  23.5 us (6%)
  blocking collectives  21 us (5%)
  matrix products  18.7 us (4%)
  between operations  16.4 us (4%)
  other arithmetic  4.55 us (1%)
    all_gather x1, waiting for transfers between devices, local(): column = lax.all_gather(packed, 'sp_1', axis=0, tiled=True)  137 us
    all_to_all x1, waiting for transfers between devices, local(): lax.all_to_all(height_back.reshape(-1, lines, part), SP, split_axis=0, co...  91.3 us
    all_to_all x1, starting transfers between devices, local(): lax.all_to_all(spread, SP, split_axis=0, concat_axis=0, tiled=True)  53.7 us
    all_to_all x1, waiting for transfers between devices, local(): lax.all_to_all(jnp.stack([column] * lax.axis_size('sp_0')), 'sp_0', 0, 0)  27.5 us
    all_to_all x1, starting transfers between devices, local(): lax.all_to_all(height_back.reshape(-1, lines, part), SP, split_axis=0, co...  25.6 us
    all_to_all x1, blocking collectives, local(): moved = lax.all_to_all(mixed, 'ch', split_axis=0, concat_axis=1, tiled=True)  18 us
    dot_general x4, matrix products, dot(): return jnp.dot(a, b, preferred_element_type=F32)  16.7 us
  transfers between devices with their start and end apart: 5, of which 3 were waited for; matrix products, arithmetic and copies ran while one was open for 5% of the time, Pallas kernels for 0%

profile of v1, /device:TPU:33, one launch (start us, length us, event | category | flops | bytes accessed | tf_op | source)
XLA Modules:
  0.0 425.2 jit_solution(15691643045250507557)
XLA Ops:
  7.4 1.3 constant_dynamic-slice_fusion
  8.7 0.7 convolution_convert_fusion.3
  9.4 1.5 copy.24
  11.0 53.7 %all-to-all-start = ((bf16[128,8,512]{2,1,0:T(8,128)(2,1)}), bf16[128,8,512]{2,1,0:T(8,128)(2,1)S(1)}, u32[]{:S(2)}, u32[]{:S(2)}) async-start(bf16[128,8,512]{2,1,0:T(8,128)(2,1)} %copy.24), calls=%async_computation | async-start | bytes 2097152 | tf_op jit(solution)/shard_map/all_to_all | solution.py:71
  65.2 1.3 dynamic-slice.1
  67.6 3.0 all-reduce.1
  71.4 137.2 %all-gather.5.cloned.1.call-done = bf16[256,2176]{1,0:T(8,128)(2,1)} async-done(((bf16[8,2176]{1,0:T(8,128)(2,1)}), bf16[256,2176]{1,0:T(8,128)(2,1)}) %all-gather.5.cloned.1.call-update) | async-done | bytes 1114128 | tf_op jit(solution)/shard_map/all_gather | solution.py:62
  208.7 1.6 copy.26
  210.3 2.4 stack.22
  212.7 5.0 %all-to-all-start.1 = ((bf16[4,256,2176]{1,2,0:T(8,128)(2,1)}), bf16[4,256,2176]{1,2,0:T(8,128)(2,1)}, u32[]{:S(2)}, u32[]{:S(2)}) async-start(bf16[4,256,2176]{1,2,0:T(8,128)(2,1)} %stack.22), calls=%async_computation.1 | async-start | bytes 8912896 | tf_op jit(solution)/shard_map/all_to_all | solution.py:64
  218.6 3.0 fusion
  221.6 5.5 %convert_element_type.98 = bf16[1024,1024]{1,0:T(8,128)(2,1)S(1)} reshape(bf16[16,64,16,64]{3,2,1,0:T(8,128)(2,1)} %fusion) | data formatting | bytes 4194304 | tf_op jit(solution)/shard_map/convert_element_type | solution.py:68
  227.1 27.5 %all-to-all-done.1 = bf16[4,256,2176]{1,2,0:T(8,128)(2,1)} async-done(((bf16[4,256,2176]{1,2,0:T(8,128)(2,1)}), bf16[4,256,2176]{1,2,0:T(8,128)(2,1)}, u32[]{:S(2)}, u32[]{:S(2)}) %all-to-all-start.1) | async-done | bytes 4456480 | tf_op jit(solution)/shard_map/all_to_all | solution.py:64
  254.6 6.5 %copy.27 = bf16[4,256,2176]{2,1,0:T(8,128)(2,1)} copy(bf16[4,256,2176]{1,2,0:T(8,128)(2,1)} %all-to-all-done.1) | data formatting | bytes 8912896 | tf_op jit(solution)/shard_map/all_to_all | solution.py:64
  261.1 5.2 %fusion.3 = bf16[1024,512]{1,0:T(8,128)(2,1)} fusion(bf16[1024,512]{1,0:T(8,128)(2,1)S(1)} %bitcast.69, bf16[1024,1024]{1,0:T(8,128)(2,1)S(1)} %convert_element_type.98, bf16[1024,1024]{1,0:T(8,128)(2,1)} %all-gather.3.cloned.1.call-done, bf16[1024,2176]{1,0:T(8,128)(2,1)} %bitcast.59), kind=kOutput, calls=%fused_computation.5 | convolution fusion | flops 2150629376 | bytes 7340032 | tf_op jit(solution)/shard_map/dot_general | solution.py:37
  266.3 3.5 fusion.12
  269.7 25.6 %all-to-all-start.2 = ((bf16[128,8,512]{2,1,0:T(8,128)(2,1)}), bf16[128,8,512]{2,1,0:T(8,128)(2,1)S(1)}, u32[]{:S(2)}, u32[]{:S(2)}) async-start(bf16[128,8,512]{2,1,0:T(8,128)(2,1)} %fusion.12), calls=%async_computation.2 | async-start | bytes 2097152 | tf_op jit(solution)/shard_map/all_to_all | solution.py:79
  295.9 1.2 fusion.70
  297.4 91.3 %all-to-all-done.2 = bf16[128,8,512]{2,1,0:T(8,128)(2,1)S(1)} async-done(((bf16[128,8,512]{2,1,0:T(8,128)(2,1)}), bf16[128,8,512]{2,1,0:T(8,128)(2,1)S(1)}, u32[]{:S(2)}, u32[]{:S(2)}) %all-to-all-start.2) | async-done | bytes 1048608 | tf_op jit(solution)/shard_map/all_to_all | solution.py:79
  388.7 1.1 fusion.15
  389.8 1.9 copy.29
  391.6 4.2 fusion.9
  395.9 18.0 %all_to_all.34 = bf16[2,512,512]{1,2,0:T(8,128)(2,1)S(1)} all-to-all(bf16[2,512,512]{1,2,0:T(8,128)(2,1)S(1)} %bitcast.65), channel_id=1, replica_groups=mesh['grp'=2,'sp_0'=4,'sp_1'=32,'ch'=2] {'ch'}, dimensions={0} | all-to-all | bytes 2097152 | tf_op jit(solution)/shard_map/all_to_all | solution.py:91
  413.9 3.8 add_convert_fusion
  (37 shorter events, 2.9 us)
Async XLA Ops:
  9.4 55.4 %copy-start.6 = (s32[256]{0:T(256)S(1)}, s32[256]{0:T(256)}, u32[]{:S(2)}) copy-start(s32[256]{0:T(256)} %param.14) | copy-start | bytes 3076
  9.4 57.7 %copy-start.2 = (bf16[4,32768]{1,0:T(4,128)(2,1)S(1)}, bf16[4,32768]{1,0:T(4,128)(2,1)}, u32[]{:S(2)}) copy-start(bf16[4,32768]{1,0:T(4,128)(2,1)} %param.13) | copy-start | bytes 786436
  9.4 61.4 %copy-start.3 = (bf16[8,1024]{1,0:T(8,128)(2,1)S(1)}, bf16[8,1024]{1,0:T(8,128)(2,1)}, u32[]{:S(2)}) copy-start(bf16[8,1024]{1,0:T(8,128)(2,1)} %param.12) | copy-start | bytes 49156
  9.4 61.4 %copy-start.4 = (bf16[8,512]{1,0:T(8,128)(2,1)S(1)}, bf16[8,512]{1,0:T(8,128)(2,1)}, u32[]{:S(2)}) copy-start(bf16[8,512]{1,0:T(8,128)(2,1)} %param.11) | copy-start | bytes 24580
  9.4 61.4 %copy-start.5 = (bf16[8,512]{1,0:T(8,128)(2,1)S(1)}, bf16[8,512]{1,0:T(8,128)(2,1)}, u32[]{:S(2)}) copy-start(bf16[8,512]{1,0:T(8,128)(2,1)} %param.10) | copy-start | bytes 24580
  11.0 199.3 %all-to-all-start = ((bf16[128,8,512]{2,1,0:T(8,128)(2,1)}), bf16[128,8,512]{2,1,0:T(8,128)(2,1)S(1)}, u32[]{:S(2)}, u32[]{:S(2)}) async-start(bf16[128,8,512]{2,1,0:T(8,128)(2,1)} %copy.24), calls=%async_computation | async-start | bytes 2097152 | tf_op jit(solution)/shard_map/all_to_all | solution.py:71
  64.7 144.0 %all-gather.5.cloned.1.call-start = ((), (), s32[]{:S(2)}) async-start(), calls=%async_computation.5 | async-start | bytes 1148928 | tf_op jit(solution)/shard_map/all_gather | solution.py:62
  210.3 2.4 copy-start
  212.7 41.9 %all-to-all-start.1 = ((bf16[4,256,2176]{1,2,0:T(8,128)(2,1)}), bf16[4,256,2176]{1,2,0:T(8,128)(2,1)}, u32[]{:S(2)}, u32[]{:S(2)}) async-start(bf16[4,256,2176]{1,2,0:T(8,128)(2,1)} %stack.22), calls=%async_computation.1 | async-start | bytes 8912896 | tf_op jit(solution)/shard_map/all_to_all | solution.py:64
  217.8 43.3 %all-gather.3.cloned.1.call-start = ((), (), s32[]{:S(2)}) async-start(), calls=%async_computation.4 | async-start | bytes 3145728 | tf_op jit(solution)/shard_map/all_gather | solution.py:73
  227.1 34.0 %copy-start.7 = (bf16[16,64,1,512]{3,1,2,0:T(8,128)(2,1)S(1)}, bf16[16,64,1,512]{3,1,2,0:T(8,128)(2,1)}, u32[]{:S(2)}) copy-start(bf16[16,64,1,512]{3,1,2,0:T(8,128)(2,1)} %param.9) | copy-start | bytes 3145732
  269.7 119.0 %all-to-all-start.2 = ((bf16[128,8,512]{2,1,0:T(8,128)(2,1)}), bf16[128,8,512]{2,1,0:T(8,128)(2,1)S(1)}, u32[]{:S(2)}, u32[]{:S(2)}) async-start(bf16[128,8,512]{2,1,0:T(8,128)(2,1)} %fusion.12), calls=%async_computation.2 | async-start | bytes 2097152 | tf_op jit(solution)/shard_map/all_to_all | solution.py:79
  395.9 18.0 %copy-start.1 = (bf16[1024,1024]{1,0:T(8,128)(2,1)S(1)}, bf16[1024,1024]{1,0:T(8,128)(2,1)}, u32[]{:S(2)}) copy-start(bf16[1024,1024]{1,0:T(8,128)(2,1)} %param.8) | copy-start | bytes 6291460
Sparse Core Ops, SparseCore 0:
  71.6 137.0 all-gather.4
Sparse Core Ops, SparseCore 1:
  220.4 38.1 all-gather.2
